TPU v7x, 32 devices: a whole 2x2x4 slice. The times are simulated.
32 devices in a mesh: dp: 4 (over y, x), vocab: 8 (over z, core).
Axes of the slice: x: 2, y: 2, z: 4, core: 2. Of those that a mesh axis runs over, the one named last changes fastest.
Arguments:
- logits: bfloat16 [32, 8, 152064], P('dp', None, 'vocab'), may hold values from -40 to 250
- draft_probs: bfloat16 [32, 8, 152064], P('dp', None, 'vocab'), may hold values from 5.9185606e-07 to 1, as said below
- draft_tokens: int32 [32, 8], P('dp'), may hold values from 0 to 152063
- draft_lengths: int32 [32], P('dp'), may hold values from 1 to 8
- owner_group: int32 [32], P('dp'), may hold values from 0 to 3, as said below
Outputs:
- correction: bfloat16 [64, 152064], P('dp', 'vocab')
- accept_ratio: float32 [64, 8], P('dp')
- expected_accepted: float32 [64], P('dp')
Inputs may be any that keep to these rules, and one draw needn't show every extreme that they name: Each row of draft_probs is a distribution over the whole vocabulary whose entries are all positive. `owner_group`: no group hands more than 4 sequences to one group; some group receives exactly 4 sequences from every group.
All inputs are finite; a program needn't handle non-finite values.
Results may differ from a plain program's by a relative error of at most 0.001.
Values may be sent and summed in bfloat16 or wider, within the bound.
A program may use at most 64 MiB of HBM per device.

v0:
```python
import jax
import jax.numpy as jnp
from jax import lax
from jax.sharding import PartitionSpec as P

mixing = 0.1


def verify(logits, draft_probs, tokens, lengths):
    scores = logits.astype(jnp.float32)
    shard_width = scores.shape[2]
    column = (
        lax.broadcasted_iota(jnp.int32, scores.shape, 2) + lax.axis_index("vocab") * shard_width
    )
    is_drafted = column == tokens[:, :, None]
    proposal = draft_probs.astype(jnp.float32)
    drafted_local = jnp.sum(jnp.where(is_drafted, proposal, 0.0), axis=2)
    top = lax.pmax(jnp.max(scores, axis=2), "vocab")
    shifted = jnp.exp(scores - top[:, :, None])
    row_total, chosen, drafted = lax.psum(
        (
            jnp.sum(shifted, axis=2),
            jnp.sum(jnp.where(is_drafted, shifted, 0.0), axis=2),
            drafted_local,
        ),
        "vocab",
    )
    target = shifted / row_total[:, :, None]
    excess = jnp.maximum(target - proposal, 0.0)
    spread = lax.psum(jnp.sum(excess, axis=2), "vocab")
    residual = (excess + mixing * target) / (spread + mixing)[:, :, None]
    position = lax.broadcasted_iota(jnp.int32, tokens.shape, 1)
    is_live = position < lengths[:, None]
    safe_draft = jnp.where(is_live, drafted, 1.0)
    accept = jnp.where(is_live, jnp.minimum(1.0, chosen / row_total / safe_draft), 0.0)
    survive = jnp.cumprod(accept, axis=1)
    before = jnp.concatenate([jnp.ones_like(survive[:, :1]), survive[:, :-1]], axis=1)
    weight = jnp.where(is_live, before * (1.0 - accept), 0.0)
    corrected = jnp.sum(weight[:, :, None] * residual, axis=1).astype(jnp.bfloat16)
    expected = jnp.sum(survive, axis=1)
    return (corrected, accept, expected)


def routing(owners, capacity, groups):
    seq_count = owners.shape[0]
    earlier = lax.broadcasted_iota(jnp.int32, (seq_count, seq_count), 1) < lax.broadcasted_iota(
        jnp.int32, (seq_count, seq_count), 0
    )
    same = owners[:, None] == owners[None, :]
    slot_rank = jnp.sum(jnp.where(same & earlier, 1, 0), axis=1)
    target_slot = owners * capacity + slot_rank
    slot_rows = lax.broadcasted_iota(jnp.int32, (groups * capacity, seq_count), 0)
    return slot_rows == target_slot[None, :]


def body(logits, draft_probs, draft_tokens, draft_lengths, owner_group):
    groups = lax.axis_size("dp")
    seq_count = owner_group.shape[0]
    capacity = max(2, 2 * seq_count // groups)
    select = routing(owner_group, capacity, groups)
    picker = select.astype(jnp.bfloat16)
    corrected, accept, expected = verify(logits, draft_probs, draft_tokens, draft_lengths)
    outgoing = jnp.dot(picker, corrected, preferred_element_type=jnp.float32).astype(jnp.bfloat16)
    correction = lax.all_to_all(outgoing, "dp", split_axis=0, concat_axis=0, tiled=True)
    sent_accept = jnp.sum(jnp.where(select[:, :, None], accept[None, :, :], 0.0), axis=1)
    sent_expected = jnp.sum(jnp.where(select, expected[None, :], 0.0), axis=1)
    accept_ratio, expected_accepted = (
        lax.all_to_all(sent_accept, "dp", split_axis=0, concat_axis=0, tiled=True),
        lax.all_to_all(sent_expected, "dp", split_axis=0, concat_axis=0, tiled=True),
    )
    return (correction, accept_ratio, expected_accepted)


def solution(mesh):
    placed = (P("dp", None, "vocab"), P("dp", None, "vocab"), P("dp", None), P("dp"), P("dp"))
    return jax.shard_map(
        body,
        mesh=mesh,
        in_specs=placed,
        out_specs=(P("dp", "vocab"), P("dp", None), P("dp")),
        check_vma=False,
    )
```

profile of v0, /device:TPU:0, one launch (start us, length us, event | category | flops | bytes accessed | tf_op | source)
XLA Modules:
  0.0 98.8 jit_solution(12494934219520476122)
XLA Ops:
  0.6 0.0 copy-start
  0.7 1.0 %select_reduce_fusion.2 = s32[8]{0:T(128)S(1)} fusion(s32[8]{0:T(128)} %param.9), kind=kLoop, calls=%fused_computation.19 | loop fusion | flops 312 | bytes 64 | tf_op jit(solution)/shard_map/reduce_sum | solution.py:50
  1.7 0.7 multiply_add_fusion
  2.3 2.2 %reduce_max.14 = bf16[8,8]{1,0:T(8,128)(2,1)S(1)} reduce(bf16[8,8,19008]{2,1,0:T(8,128)(2,1)} %param.5, bf16[]{:T(256)} %constant.14.clone.1), dimensions={2}, to_apply=%region_1.2 | reduce | flops 1216448 | bytes 2433154 | tf_op jit(solution)/shard_map/reduce_max | solution.py:18
  4.5 18.1 %pmax.7 = f32[8,8]{1,0:T(8,128)S(1)} all-reduce(bf16[8,8]{1,0:T(8,128)(2,1)S(1)} %reduce_max.14), channel_id=1, replica_groups=mesh['dp'=4,'vocab'=8] {'vocab'}, use_global_device_ids=true, to_apply=%region_2.3 | all-reduce | flops 64 | bytes 384 | tf_op jit(solution)/shard_map/pmax | solution.py:18
  22.6 1.7 %fusion.1 = (f32[8,8]{1,0:T(8,128)S(1)}, f32[8,8]{1,0:T(8,128)S(1)}) fusion(bf16[8,8,19008]{2,1,0:T(8,128)(2,1)S(1)} %copy-done, f32[8,8]{1,0:T(8,128)S(1)} %pmax.7, s32[8,8]{1,0:T(8,128)S(1)} %copy-done.1, s32[19008]{0:T(1024)S(1)} %iota_add_fusion), kind=kLoop, calls=%fused_computation.5 | loop fusion | flops 7298944 | bytes 2510080 | tf_op jit(solution)/shard_map/reduce_sum | solution.py:23
  24.3 13.6 %psum.29 = f32[8,8]{1,0:T(8,128)S(1)} all-reduce(f32[8,8]{1,0:T(8,128)S(1)} %get-tuple-element.13), channel_id=1, replica_groups=mesh['dp'=4,'vocab'=8] {'vocab'}, use_global_device_ids=true, to_apply=%region_6.7 | all-reduce | flops 64 | bytes 512 | tf_op jit(solution)/shard_map/psum | solution.py:20
  37.9 3.9 %fusion.2 = (f32[8,8]{1,0:T(8,128)S(1)}, f32[8,8]{1,0:T(8,128)S(1)}) fusion(bf16[8,8,19008]{2,1,0:T(8,128)(2,1)} %param.6, s32[8,8]{1,0:T(8,128)S(1)} %copy-done.1, s32[19008]{0:T(1024)S(1)} %iota_add_fusion, f32[8,8]{1,0:T(8,128)S(1)} %psum.29, f32[8,8]{1,0:T(8,128)S(1)} %pmax.7, bf16[8,8,19008]{2,1,0:T(8,128)(2,1)S(1)} %copy-done), kind=kLoop, calls=%fused_computation.6 | loop fusion | flops 12164992 | bytes 4943360 | tf_op jit(solution)/shard_map/reduce_sum | solution.py:17
  41.8 25.9 %all-reduce.1 = (f32[8,8]{1,0:T(8,128)S(1)}, f32[8,8]{1,0:T(8,128)S(1)}, f32[8,8]{1,0:T(8,128)S(1)}) all-reduce(f32[8,8]{1,0:T(8,128)S(1)} %get-tuple-element.15, f32[8,8]{1,0:T(8,128)S(1)} %get-tuple-element.12, f32[8,8]{1,0:T(8,128)S(1)} %get-tuple-element.14), channel_id=1, replica_groups=mesh['dp'=4,'vocab'=8] {'vocab'}, use_global_device_ids=true, to_apply=%region_11.12 | all-reduce | flops 192 | bytes 1536 | tf_op jit(solution)/shard_map/psum | solution.py:30
  67.7 0.1 minimum_select_fusion
  67.8 0.2 reduce_window.9
  68.0 0.1 reduce_sum.88
  68.1 0.1 select_reduce_fusion.1
  68.2 0.7 all_to_all.30
  68.8 3.7 %all-to-all-start.2 = ((f32[4,4,1]{1,2,0:T(1,128)}), f32[4,4,1]{1,2,0:T(1,128)S(1)}, u32[]{:S(2)}, u32[]{:S(2)}) async-start(f32[4,4,1]{1,2,0:T(1,128)} %bitcast.2), calls=%async_computation.2 | async-start | bytes 4096 | tf_op jit(solution)/shard_map/all_to_all | solution.py:69
  72.6 0.1 iota_compare_fusion.2
  72.6 0.1 select_reduce_fusion
  72.7 0.1 multiply_select_fusion
  72.8 0.7 copy.11
  73.5 4.8 %multiply_reduce_fusion = bf16[8,19008]{1,0:T(8,128)(2,1)S(1)} fusion(bf16[8,8,19008]{2,1,0:T(8,128)(2,1)} %param.6, bf16[8,8,19008]{2,1,0:T(8,128)(2,1)S(1)} %copy-done, f32[8,8]{1,0:T(8,128)S(1)} %get-tuple-element.20, f32[8,8]{1,0:T(8,128)S(1)} %psum.29, f32[8,8]{1,0:T(8,128)S(1)} %multiply_select_fusion, f32[8,8]{1,0:T(8,128)S(1)} %pmax.7), kind=kLoop, calls=%fused_computation.7 | loop fusion | flops 13229568 | bytes 5171200 | tf_op jit(solution)/shard_map/reduce_sum | solution.py:39
  78.3 0.0 all-to-all-done.2
  78.3 4.2 %all-to-all-start.1 = ((f32[4,4,8]{2,1,0:T(4,128)}), f32[4,4,8]{2,1,0:T(4,128)S(1)}, u32[]{:S(2)}, u32[]{:S(2)}) async-start(f32[4,4,8]{2,1,0:T(4,128)} %bitcast), calls=%async_computation.1 | async-start | bytes 16384 | tf_op jit(solution)/shard_map/all_to_all | solution.py:68
  82.5 0.4 convolution_convert_fusion
  82.9 1.0 all_to_all.24
  83.9 3.3 %all-to-all-done.1 = f32[4,4,8]{2,1,0:T(4,128)S(1)} async-done(((f32[4,4,8]{2,1,0:T(4,128)}), f32[4,4,8]{2,1,0:T(4,128)S(1)}, u32[]{:S(2)}, u32[]{:S(2)}) %all-to-all-start.1) | async-done | bytes 544 | tf_op jit(solution)/shard_map/all_to_all | solution.py:68
  87.2 3.5 %all-to-all-start = ((bf16[4,4,19008]{2,1,0:T(4,128)(2,1)}), bf16[4,4,19008]{2,1,0:T(4,128)(2,1)S(1)}, u32[]{:S(2)}, u32[]{:S(2)}) async-start(bf16[4,4,19008]{2,1,0:T(4,128)(2,1)} %all_to_all.24), calls=%async_computation | async-start | bytes 1220608 | tf_op jit(solution)/shard_map/all_to_all | solution.py:64
  90.6 0.5 broadcast.32
  91.2 0.7 reduce.4
  91.8 0.6 all_to_all.32
  92.4 0.7 copy.13
  93.1 4.6 %all-to-all-done = bf16[4,4,19008]{2,1,0:T(4,128)(2,1)S(1)} async-done(((bf16[4,4,19008]{2,1,0:T(4,128)(2,1)}), bf16[4,4,19008]{2,1,0:T(4,128)(2,1)S(1)}, u32[]{:S(2)}, u32[]{:S(2)}) %all-to-all-start) | async-done | bytes 608288 | tf_op jit(solution)/shard_map/all_to_all | solution.py:64
  97.7 1.1 %all_to_all.26 = bf16[16,19008]{1,0:T(8,128)(2,1)} reshape(bf16[4,4,19008]{2,1,0:T(4,128)(2,1)S(1)} %all-to-all-done) | data formatting | bytes 1216512 | tf_op jit(solution)/shard_map/all_to_all | solution.py:64
  (6 shorter events, 0.0 us)
Async XLA Ops:
  0.6 22.0 %copy-start = (bf16[8,8,19008]{2,1,0:T(8,128)(2,1)S(1)}, bf16[8,8,19008]{2,1,0:T(8,128)(2,1)}, u32[]{:S(2)}) copy-start(bf16[8,8,19008]{2,1,0:T(8,128)(2,1)} %param.5) | copy-start | bytes 7299076
  0.6 22.0 %copy-start.1 = (s32[8,8]{1,0:T(8,128)S(1)}, s32[8,8]{1,0:T(8,128)}, u32[]{:S(2)}) copy-start(s32[8,8]{1,0:T(8,128)} %param.7) | copy-start | bytes 772
  37.9 29.8 %copy-start.2 = (s32[8]{0:T(128)S(1)}, s32[8]{0:T(128)}, u32[]{:S(2)}) copy-start(s32[8]{0:T(128)} %param.8) | copy-start | bytes 100
  68.8 9.4 %all-to-all-start.2 = ((f32[4,4,1]{1,2,0:T(1,128)}), f32[4,4,1]{1,2,0:T(1,128)S(1)}, u32[]{:S(2)}, u32[]{:S(2)}) async-start(f32[4,4,1]{1,2,0:T(1,128)} %bitcast.2), calls=%async_computation.2 | async-start | bytes 4096 | tf_op jit(solution)/shard_map/all_to_all | solution.py:69
  78.3 8.9 %all-to-all-start.1 = ((f32[4,4,8]{2,1,0:T(4,128)}), f32[4,4,8]{2,1,0:T(4,128)S(1)}, u32[]{:S(2)}, u32[]{:S(2)}) async-start(f32[4,4,8]{2,1,0:T(4,128)} %bitcast), calls=%async_computation.1 | async-start | bytes 16384 | tf_op jit(solution)/shard_map/all_to_all | solution.py:68
  87.2 10.5 %all-to-all-start = ((bf16[4,4,19008]{2,1,0:T(4,128)(2,1)}), bf16[4,4,19008]{2,1,0:T(4,128)(2,1)S(1)}, u32[]{:S(2)}, u32[]{:S(2)}) async-start(bf16[4,4,19008]{2,1,0:T(4,128)(2,1)} %all_to_all.24), calls=%async_computation | async-start | bytes 1220608 | tf_op jit(solution)/shard_map/all_to_all | solution.py:64
where the time goes:
time: 99.2 us; the launch traced here: 98.8 us
  blocking collectives  57.6 us (58%)
  other arithmetic  15.6 us (16%)
  starting transfers between devices  11.4 us (11%)
  waiting for transfers between devices  7.9 us (8%)
  local copies, waits for them, and re-layouts  5.16 us (5%)
    psum x1, blocking collectives, verify(): spread = lax.psum(jnp.sum(excess, axis=2), 'vocab')  25.9 us
    pmax x1, blocking collectives, verify(): top = lax.pmax(jnp.max(scores, axis=2), 'vocab')  18.1 us
    psum x1, blocking collectives, verify(): lax.psum((jnp.sum(shifted, axis=2), jnp.sum(jnp.where(is_drafted, shifted...  13.6 us
    reduce_sum x1, other arithmetic, verify(): jnp.sum(weight[:, :, None] * residual, axis=1).astype(jnp.bfloat16)  4.79 us
    all_to_all x1, waiting for transfers between devices, body(): lax.all_to_all(outgoing, 'dp', split_axis=0, concat_axis=0, tiled=True)  4.61 us
    all_to_all x1, starting transfers between devices, body(): lax.all_to_all(sent_accept, 'dp', split_axis=0, concat_axis=0, tiled=True)  4.2 us
    reduce_sum x1, other arithmetic, verify(): drafted_local = jnp.sum(jnp.where(is_drafted, proposal, 0.0), axis=2)  3.89 us
    all_to_all x1, starting transfers between devices, body(): lax.all_to_all(sent_expected, 'dp', split_axis=0, concat_axis=0, tiled=True)  3.72 us
  transfers between devices with their start and end apart: 3, of which 2 were waited for; matrix products, arithmetic and copies ran while one was open for 8% of the time, Pallas kernels for 0%

commit v1 on v0

--- a/solution.py
+++ b/solution.py
@@ -27,7 +27,7 @@
     )
     target = shifted / row_total[:, :, None]
     excess = jnp.maximum(target - proposal, 0.0)
-    spread = lax.psum(jnp.sum(excess, axis=2), "vocab")
+    spread = jnp.sum(lax.all_gather(jnp.sum(excess, axis=2), "vocab"), axis=0)
     residual = (excess + mixing * target) / (spread + mixing)[:, :, None]
     position = lax.broadcasted_iota(jnp.int32, tokens.shape, 1)
     is_live = position < lengths[:, None]

time: 99.2 us -> 103 us (1.038)
  blocking collectives: 57.6 us -> 59.6 us
  waiting for transfers between devices: 7.9 us -> 9.12 us
    psum x1 -> x0, blocking collectives: 25.9 us -> none  [verify(): spread = lax.psum(jnp.sum(excess, axis=2), 'vocab')]
    all_gather x0 -> x1, blocking collectives: none -> 14.1 us  [verify(): spread = jnp.sum(lax.all_gather(jnp.sum(excess, axis=2), 'vocab'), axis=0)]
    psum x1 -> x2, blocking collectives: 13.6 us -> 27.5 us  [verify(): lax.psum((jnp.sum(shifted, axis=2), jnp.sum(jnp.where(is_drafted, shifted...]
    all_to_all x1, waiting for transfers between devices: 4.61 us -> 5.83 us  [body(): lax.all_to_all(outgoing, 'dp', split_axis=0, concat_axis=0, tiled=True)]
where the time goes in v1:
time: 103 us; the launch traced here: 102 us
  blocking collectives  59.6 us (58%)
  other arithmetic  15.6 us (15%)
  starting transfers between devices  11.4 us (11%)
  waiting for transfers between devices  9.12 us (9%)
  local copies, waits for them, and re-layouts  5.16 us (5%)
    psum x2, blocking collectives, verify(): lax.psum((jnp.sum(shifted, axis=2), jnp.sum(jnp.where(is_drafted, shifted...  27.5 us
    pmax x1, blocking collectives, verify(): top = lax.pmax(jnp.max(scores, axis=2), 'vocab')  18.1 us
    all_gather x1, blocking collectives, verify(): spread = jnp.sum(lax.all_gather(jnp.sum(excess, axis=2), 'vocab'), axis=0)  14.1 us
    all_to_all x1, waiting for transfers between devices, body(): lax.all_to_all(outgoing, 'dp', split_axis=0, concat_axis=0, tiled=True)  5.83 us
    reduce_sum x1, other arithmetic, verify(): jnp.sum(weight[:, :, None] * residual, axis=1).astype(jnp.bfloat16)  4.8 us
    all_to_all x1, starting transfers between devices, body(): lax.all_to_all(sent_accept, 'dp', split_axis=0, concat_axis=0, tiled=True)  4.2 us
    reduce_sum x1, other arithmetic, verify(): drafted_local = jnp.sum(jnp.where(is_drafted, proposal, 0.0), axis=2)  3.89 us
    all_to_all x1, starting transfers between devices, body(): lax.all_to_all(sent_expected, 'dp', split_axis=0, concat_axis=0, tiled=True)  3.72 us
  transfers between devices with their start and end apart: 3, of which 2 were waited for; matrix products, arithmetic and copies ran while one was open for 8% of the time, Pallas kernels for 0%

profile of v1, /device:TPU:0, one launch (start us, length us, event | category | flops | bytes accessed | tf_op | source)
XLA Modules:
  0.0 102.1 jit_solution(3289026962107947196)
XLA Ops:
  0.6 0.0 copy-start
  0.7 1.0 select_reduce_fusion.2
  1.7 0.7 multiply_add_fusion
  2.3 2.2 %reduce_max.14 = bf16[8,8]{1,0:T(8,128)(2,1)S(1)} reduce(bf16[8,8,19008]{2,1,0:T(8,128)(2,1)} %param.5, bf16[]{:T(256)} %constant.14.clone.1), dimensions={2}, to_apply=%region_1.2 | reduce | flops 1216448 | bytes 2433154 | tf_op jit(solution)/shard_map/reduce_max | solution.py:18
  4.5 18.1 %pmax.7 = f32[8,8]{1,0:T(8,128)S(1)} all-reduce(bf16[8,8]{1,0:T(8,128)(2,1)S(1)} %reduce_max.14), channel_id=1, replica_groups=mesh['dp'=4,'vocab'=8] {'vocab'}, use_global_device_ids=true, to_apply=%region_2.3 | all-reduce | flops 64 | bytes 384 | tf_op jit(solution)/shard_map/pmax | solution.py:18
  22.6 1.7 %fusion.1 = (f32[8,8]{1,0:T(8,128)S(1)}, f32[8,8]{1,0:T(8,128)S(1)}) fusion(bf16[8,8,19008]{2,1,0:T(8,128)(2,1)S(1)} %copy-done, f32[8,8]{1,0:T(8,128)S(1)} %pmax.7, s32[8,8]{1,0:T(8,128)S(1)} %copy-done.1, s32[19008]{0:T(1024)S(1)} %iota_add_fusion), kind=kLoop, calls=%fused_computation.5 | loop fusion | flops 7298944 | bytes 2510080 | tf_op jit(solution)/shard_map/reduce_sum | solution.py:23
  24.3 13.6 %psum.22 = f32[8,8]{1,0:T(8,128)S(1)} all-reduce(f32[8,8]{1,0:T(8,128)S(1)} %get-tuple-element.13), channel_id=1, replica_groups=mesh['dp'=4,'vocab'=8] {'vocab'}, use_global_device_ids=true, to_apply=%region_6.7 | all-reduce | flops 64 | bytes 512 | tf_op jit(solution)/shard_map/psum | solution.py:20
  37.9 3.9 %fusion.2 = (f32[8,8]{1,0:T(8,128)S(1)}, f32[8,8]{1,0:T(8,128)S(1)}) fusion(bf16[8,8,19008]{2,1,0:T(8,128)(2,1)} %param.6, s32[8,8]{1,0:T(8,128)S(1)} %copy-done.1, s32[19008]{0:T(1024)S(1)} %iota_add_fusion, f32[8,8]{1,0:T(8,128)S(1)} %psum.22, f32[8,8]{1,0:T(8,128)S(1)} %pmax.7, bf16[8,8,19008]{2,1,0:T(8,128)(2,1)S(1)} %copy-done), kind=kLoop, calls=%fused_computation.6 | loop fusion | flops 12164992 | bytes 4943360 | tf_op jit(solution)/shard_map/reduce_sum | solution.py:17
  41.8 13.9 %all-reduce.1 = (f32[8,8]{1,0:T(8,128)S(1)}, f32[8,8]{1,0:T(8,128)S(1)}) all-reduce(f32[8,8]{1,0:T(8,128)S(1)} %get-tuple-element.12, f32[8,8]{1,0:T(8,128)S(1)} %get-tuple-element.14), channel_id=1, replica_groups=mesh['dp'=4,'vocab'=8] {'vocab'}, use_global_device_ids=true, to_apply=%region_4.5 | all-reduce | flops 128 | bytes 1024 | tf_op jit(solution)/shard_map/psum | solution.py:20
  55.7 0.1 minimum_select_fusion
  55.8 0.2 reduce_window.9
  56.0 0.1 reduce_sum.98
  56.1 0.1 select_reduce_fusion.1
  56.2 0.7 all_to_all.30
  56.8 3.7 %all-to-all-start.2 = ((f32[4,4,1]{1,2,0:T(1,128)}), f32[4,4,1]{1,2,0:T(1,128)S(1)}, u32[]{:S(2)}, u32[]{:S(2)}) async-start(f32[4,4,1]{1,2,0:T(1,128)} %bitcast.3), calls=%async_computation.2 | async-start | bytes 4096 | tf_op jit(solution)/shard_map/all_to_all | solution.py:69
  60.6 0.1 iota_compare_fusion.2
  60.6 0.1 select_reduce_fusion
  60.7 0.1 multiply_select_fusion
  60.8 0.7 copy.11
  61.5 14.1 %all-gather = f32[64,8]{1,0:T(8,128)S(1)} all-gather(f32[8,8]{1,0:T(8,128)S(1)} %get-tuple-element.15), channel_id=2, replica_groups=mesh['dp'=4,'vocab'=8] {'vocab'}, dimensions={0}, use_global_device_ids=true | all-gather | bytes 2304 | tf_op jit(solution)/shard_map/all_gather | solution.py:30
  75.6 4.8 %multiply_reduce_fusion = bf16[8,19008]{1,0:T(8,128)(2,1)S(1)} fusion(bf16[8,8,19008]{2,1,0:T(8,128)(2,1)} %param.6, bf16[8,8,19008]{2,1,0:T(8,128)(2,1)S(1)} %copy-done, f32[8,8]{1,0:T(8,128)S(1)} %broadcast_add_fusion, f32[8,8]{1,0:T(8,128)S(1)} %psum.22, f32[8,8]{1,0:T(8,128)S(1)} %multiply_select_fusion, f32[8,8]{1,0:T(8,128)S(1)} %pmax.7), kind=kLoop, calls=%fused_computation.7 | loop fusion | flops 13229568 | bytes 5171200 | tf_op jit(solution)/shard_map/reduce_sum | solution.py:39
  80.4 4.2 %all-to-all-start.1 = ((f32[4,4,8]{2,1,0:T(4,128)}), f32[4,4,8]{2,1,0:T(4,128)S(1)}, u32[]{:S(2)}, u32[]{:S(2)}) async-start(f32[4,4,8]{2,1,0:T(4,128)} %bitcast.1), calls=%async_computation.1 | async-start | bytes 16384 | tf_op jit(solution)/shard_map/all_to_all | solution.py:68
  84.6 0.4 convolution_convert_fusion
  85.0 1.0 all_to_all.24
  86.0 3.3 %all-to-all-done.1 = f32[4,4,8]{2,1,0:T(4,128)S(1)} async-done(((f32[4,4,8]{2,1,0:T(4,128)}), f32[4,4,8]{2,1,0:T(4,128)S(1)}, u32[]{:S(2)}, u32[]{:S(2)}) %all-to-all-start.1) | async-done | bytes 544 | tf_op jit(solution)/shard_map/all_to_all | solution.py:68
  89.3 3.5 %all-to-all-start = ((bf16[4,4,19008]{2,1,0:T(4,128)(2,1)}), bf16[4,4,19008]{2,1,0:T(4,128)(2,1)S(1)}, u32[]{:S(2)}, u32[]{:S(2)}) async-start(bf16[4,4,19008]{2,1,0:T(4,128)(2,1)} %all_to_all.24), calls=%async_computation | async-start | bytes 1220608 | tf_op jit(solution)/shard_map/all_to_all | solution.py:64
  92.8 0.5 broadcast.35
  93.3 0.7 reduce.4
  93.9 0.6 all_to_all.32
  94.5 0.7 copy.13
  95.2 5.8 %all-to-all-done = bf16[4,4,19008]{2,1,0:T(4,128)(2,1)S(1)} async-done(((bf16[4,4,19008]{2,1,0:T(4,128)(2,1)}), bf16[4,4,19008]{2,1,0:T(4,128)(2,1)S(1)}, u32[]{:S(2)}, u32[]{:S(2)}) %all-to-all-start) | async-done | bytes 608288 | tf_op jit(solution)/shard_map/all_to_all | solution.py:64
  101.0 1.1 %all_to_all.26 = bf16[16,19008]{1,0:T(8,128)(2,1)} reshape(bf16[4,4,19008]{2,1,0:T(4,128)(2,1)S(1)} %all-to-all-done) | data formatting | bytes 1216512 | tf_op jit(solution)/shard_map/all_to_all | solution.py:64
  (9 shorter events, 0.0 us)
Async XLA Ops:
  0.6 22.0 %copy-start = (bf16[8,8,19008]{2,1,0:T(8,128)(2,1)S(1)}, bf16[8,8,19008]{2,1,0:T(8,128)(2,1)}, u32[]{:S(2)}) copy-start(bf16[8,8,19008]{2,1,0:T(8,128)(2,1)} %param.5) | copy-start | bytes 7299076
  0.6 22.0 %copy-start.1 = (s32[8,8]{1,0:T(8,128)S(1)}, s32[8,8]{1,0:T(8,128)}, u32[]{:S(2)}) copy-start(s32[8,8]{1,0:T(8,128)} %param.7) | copy-start | bytes 772
  37.9 17.8 %copy-start.2 = (s32[8]{0:T(128)S(1)}, s32[8]{0:T(128)}, u32[]{:S(2)}) copy-start(s32[8]{0:T(128)} %param.8) | copy-start | bytes 100
  56.8 23.5 %all-to-all-start.2 = ((f32[4,4,1]{1,2,0:T(1,128)}), f32[4,4,1]{1,2,0:T(1,128)S(1)}, u32[]{:S(2)}, u32[]{:S(2)}) async-start(f32[4,4,1]{1,2,0:T(1,128)} %bitcast.3), calls=%async_computation.2 | async-start | bytes 4096 | tf_op jit(solution)/shard_map/all_to_all | solution.py:69
  80.4 8.9 %all-to-all-start.1 = ((f32[4,4,8]{2,1,0:T(4,128)}), f32[4,4,8]{2,1,0:T(4,128)S(1)}, u32[]{:S(2)}, u32[]{:S(2)}) async-start(f32[4,4,8]{2,1,0:T(4,128)} %bitcast.1), calls=%async_computation.1 | async-start | bytes 16384 | tf_op jit(solution)/shard_map/all_to_all | solution.py:68
  89.3 11.8 %all-to-all-start = ((bf16[4,4,19008]{2,1,0:T(4,128)(2,1)}), bf16[4,4,19008]{2,1,0:T(4,128)(2,1)S(1)}, u32[]{:S(2)}, u32[]{:S(2)}) async-start(bf16[4,4,19008]{2,1,0:T(4,128)(2,1)} %all_to_all.24), calls=%async_computation | async-start | bytes 1220608 | tf_op jit(solution)/shard_map/all_to_all | solution.py:64
